TPU v7x, 256 devices: a whole 4x4x8 slice. The times are simulated.
256 devices in a mesh: src: 4 (over x), blk: 64 (over y, z, core).
Axes of the slice: x: 4, y: 4, z: 8, core: 2. Of those that a mesh axis runs over, the one named last changes fastest.
Arguments:
- values: float32 [4, 4096, 32, 128], P('src', 'blk'), may hold values from -0.25 to 0.25
- diagonal: float32 [4, 4096, 128], P('src', 'blk'), may hold values from 0.55 to 0.95
- rhs_parts: float32 [4, 4096, 128], P('src', 'blk'), may hold values from -24 to 24
- owner_map: int32 [4096, 128], P('blk'), may hold values from 0 to 3
- columns: int32 [4096, 32, 128], P('blk'), may hold values from 0 to 1073741823
- destination: int32 [4096, 1], P('blk'), may hold values from 0 to 63; in each aligned block of 64 rows (0 to 63, 64 to 127, ...) at most 2 rows name the same one
- order_keys: int32 [4096], P('blk'), may hold values from 0 to 4095, each once
Outputs:
- solution: float32 [4096, 128], P('blk')
Inputs may be any that keep to these rules, and one draw needn't show every extreme that they name: `destination`: among the row blocks of one index of blk no owner is named more than 2 times, some owner is named exactly 2 times, and every owner is named by some block. `order_keys`: each key appears once.
All inputs are finite; a program needn't handle non-finite values.
Results may differ from a plain program's by a relative error of at most 0.0003.
Values sent between devices are 32-bit elements; how exact they have to be, the bound alone decides.
A program may use at most 64 MiB of HBM per device.

v0:
```python
import math

import jax
import jax.numpy as jnp
from jax import lax
from jax.sharding import PartitionSpec as P

SWEEPS = 3


def copy_for_each(value, axis):
    copies = jnp.broadcast_to(value, (lax.axis_size(axis), *value.shape))
    return lax.all_to_all(copies, axis, split_axis=0, concat_axis=0, tiled=True)


def taken_together(value, axis):
    everything = copy_for_each(value, axis)
    return jnp.sum(everything, axis=0)


def together(arrays, axis):
    ends = [0]
    for a in arrays:
        ends.append(ends[-1] + a.size)
    so_far = taken_together(jnp.concatenate([a.ravel() for a in arrays]), axis)
    return tuple((so_far[b:e].reshape(a.shape) for a, b, e in zip(arrays, ends, ends[1:])))


def in_one_piece(arrays, axis, split_dim, concat_dim, along):
    widths = [math.prod(a.shape[along:]) for a in arrays]
    both = jnp.concatenate(
        [a.reshape(*a.shape[:along], w) for a, w in zip(arrays, widths)], axis=along
    )
    whole = lax.all_to_all(both, axis, split_axis=split_dim, concat_axis=concat_dim, tiled=True)
    parts = jnp.split(whole, [sum(widths[:k]) for k in range(1, len(widths))], axis=along)
    return tuple((b.reshape(*whole.shape[:along], *a.shape[along:]) for a, b in zip(arrays, parts)))


def tile_matrix(block_vals, block_cols, tile_rows):
    slot_count = block_vals.shape[0]
    stored = block_vals.shape[1]
    groups = 8
    lanes = jnp.remainder(block_cols, 2 * tile_rows)
    targets = jnp.arange(2 * tile_rows, dtype=jnp.int32)
    grouped_vals = block_vals.reshape(groups, slot_count // groups, stored, tile_rows)
    grouped_lanes = lanes.reshape(groups, slot_count // groups, stored, tile_rows)

    def build(pair):
        group_vals, group_lanes = pair
        picked = jnp.where(group_lanes[..., None] == targets, group_vals[..., None], 0.0)
        return jnp.sum(picked, axis=1)

    dense = lax.map(build, (grouped_vals, grouped_lanes))
    return dense.reshape(slot_count, tile_rows, 2 * tile_rows)


def on_device(values, diagonal, rhs_parts, owner_map, columns, destination, order_keys):
    owners = lax.axis_size("blk")
    part_count = lax.axis_size("src")
    tile_count = destination.shape[0]
    stored = values.shape[2]
    tile_rows = values.shape[3]
    per_peer = 2 * tile_count // owners
    slot_count = owners * per_peer
    owner_of = destination[:, 0]
    tile_ids = jnp.arange(tile_count, dtype=jnp.int32)
    slot_ids = jnp.arange(slot_count, dtype=jnp.int32)
    earlier = (owner_of[None, :] == owner_of[:, None]) & (tile_ids[None, :] < tile_ids[:, None])
    position = jnp.sum(earlier, axis=1)
    slot_of = owner_of * per_peer + position
    slot_hits = slot_of[None, :] == slot_ids[:, None]
    filled = jnp.any(slot_hits, axis=1)
    source_tile = jnp.sum(jnp.where(slot_hits, tile_ids[None, :], 0), axis=1)
    is_owned = owner_map == lax.axis_index("src")
    own_rhs = jnp.where(is_owned, rhs_parts[0], 0.0)
    send_vals = jnp.where(filled[:, None, None], values[0][source_tile], 0.0)
    send_diag = jnp.where(filled[:, None], diagonal[0][source_tile], 0.0)
    send_rhs = jnp.where(filled[:, None], own_rhs[source_tile], 0.0)
    send_cols = columns[source_tile]
    send_keys = jnp.where(filled, order_keys[source_tile], -1)
    quarter = stored // part_count
    part_vals = lax.psum_scatter(send_vals, "src", scatter_dimension=1, tiled=True)
    sum_diag, sum_rhs = together((send_diag, send_rhs), "src")
    part_cols = lax.dynamic_slice_in_dim(send_cols, lax.axis_index("src") * quarter, quarter, 1)
    got_vals, got_diag, got_rhs = in_one_piece((part_vals, sum_diag, sum_rhs), "blk", 0, 0, 1)
    got_cols, got_keys = in_one_piece((part_cols, send_keys), "blk", 0, 0, 1)
    is_live = got_keys >= 0
    tile_total = jnp.sum(is_live)
    smaller = is_live[None, :] & (got_keys[None, :] < got_keys[:, None])
    tile_rank = jnp.sum(smaller, axis=1)
    rank_hits = is_live[None, :] & (tile_rank[None, :] == slot_ids[:, None])
    holder = jnp.sum(jnp.where(rank_hits, slot_ids[None, :], 0), axis=1)
    occupied = slot_ids < tile_total
    block_vals = jnp.where(occupied[:, None, None], got_vals[holder], 0.0)
    block_cols = got_cols[holder]
    right_side = jnp.where(occupied[:, None], got_rhs[holder], 0.0)
    block_diag = jnp.where(occupied[:, None], got_diag[holder], 1.0)
    dense = tile_matrix(block_vals, block_cols, tile_rows)
    following = jnp.remainder(slot_ids + 1, tile_total)
    iterate = jnp.zeros((slot_count, tile_rows), jnp.float32)
    for sweep_index in range(SWEEPS):
        nearby = jnp.concatenate([iterate, iterate[following]], axis=1)
        partial_sum = jnp.sum(dense * nearby[:, None, :], axis=2)
        summed = taken_together(partial_sum, "src")
        iterate = jnp.where(occupied[:, None], (right_side - summed) / block_diag, 0.0)
    in_slots = jnp.where(is_live[:, None], iterate[tile_rank], 0.0)
    returned = lax.all_to_all(in_slots, "blk", split_axis=0, concat_axis=0, tiled=True)
    return returned[slot_of]


def solution(mesh):
    placed = (
        P("src", "blk", None, None),
        P("src", "blk", None),
        P("src", "blk", None),
        P("blk", None),
        P("blk", None, None),
        P("blk", None),
        P("blk"),
    )
    return jax.shard_map(
        on_device, mesh=mesh, in_specs=placed, out_specs=P("blk", None), check_vma=False
    )
```

profile of v0, /device:TPU:1, one launch (start us, length us, event | category | flops | bytes accessed | tf_op | source)
XLA Modules:
  0.0 238.5 jit_solution(7063497085734993261)
XLA Ops:
  9.2 1.6 broadcast_select_fusion
  14.8 4.8 %all-to-all-start.1 = ((f32[4,1,32768]{2,1,0:T(1,128)}), f32[4,1,32768]{2,1,0:T(1,128)}, u32[]{:S(2)}, u32[]{:S(2)}) async-start(f32[4,1,32768]{2,1,0:T(1,128)} %broadcast_in_dim.197), calls=%async_computation.2 | async-start | bytes 1048576 | tf_op jit(solution)/shard_map/all_to_all | solution.py:13
  19.6 1.6 gather_fusion.1
  21.5 1.9 gather_fusion
  26.7 18.4 %all-to-all-start = ((s32[64,2,1025]{2,1,0:T(2,128)}), s32[64,2,1025]{2,1,0:T(2,128)S(1)}, u32[]{:S(2)}, u32[]{:S(2)}) async-start(s32[64,2,1025]{2,1,0:T(2,128)} %pad_add_fusion), calls=%async_computation | async-start | bytes 1179648 | tf_op jit(solution)/shard_map/all_to_all | solution.py:34
  46.6 17.1 %all-to-all-done = s32[64,2,1025]{2,1,0:T(2,128)S(1)} async-done(((s32[64,2,1025]{2,1,0:T(2,128)}), s32[64,2,1025]{2,1,0:T(2,128)S(1)}, u32[]{:S(2)}, u32[]{:S(2)}) %all-to-all-start) | async-done | bytes 524832 | tf_op jit(solution)/shard_map/all_to_all | solution.py:34
  68.6 6.3 %all-to-all-start.2 = ((f32[64,2,1280]{2,1,0:T(2,128)}), f32[64,2,1280]{2,1,0:T(2,128)S(1)}, u32[]{:S(2)}, u32[]{:S(2)}) async-start(f32[64,2,1280]{2,1,0:T(2,128)} %pad_maximum_fusion), calls=%async_computation.3 | async-start | bytes 1310720 | tf_op jit(solution)/shard_map/all_to_all | solution.py:34
  78.7 16.4 %all-to-all-done.2 = f32[64,2,1280]{2,1,0:T(2,128)S(1)} async-done(((f32[64,2,1280]{2,1,0:T(2,128)}), f32[64,2,1280]{2,1,0:T(2,128)S(1)}, u32[]{:S(2)}, u32[]{:S(2)}) %all-to-all-start.2) | async-done | bytes 655392 | tf_op jit(solution)/shard_map/all_to_all | solution.py:34
  96.6 57.8 %while.11 = (s32[]{:T(128)}, f32[8,16,128,256]{3,2,1,0:T(8,128)}, s32[8,16,8,128]{3,2,1,0:T(8,128)S(1)}, f32[8,16,8,128]{3,2,1,0:T(8,128)S(1)}, s32[]{:T(128)}) while((s32[]{:T(128)}, f32[8,16,128,256]{3,2,1,0:T(8,128)}, s32[8,16,8,128]{3,2,1,0:T(8,128)S(1)}, f32[8,16,8,128]{3,2,1,0:T(8,128)S(1)}, s32[]{:T(128)}) %tuple.24), condition=%wide.region_10.11_spmd.clone, body=%wide.region_8.10_spmd.clone.sunk | while | flops 12058626 | bytes 6684753 | solution.py:53
  96.7 5.7 %select_reduce_fusion.4 = f32[16,128,256]{2,1,0:T(8,128)S(1)} fusion(f32[16,8,128]{2,1,0:T(8,128)S(1)} %dynamic-slice_bitcast_fusion.4, s32[16,8,128]{2,1,0:T(8,128)S(1)} %dynamic-slice_bitcast_fusion.5), kind=kLoop, calls=%fused_computation.16.clone.1 | loop fusion | flops 12058624 | bytes 2228224 | tf_op jit(solution)/shard_map/while/body/eval_jaxpr/reduce_sum | solution.py:51
  102.3 1.6 bitcast_dynamic-update-slice_fusion.2
  103.9 5.7 %select_reduce_fusion.4 = f32[16,128,256]{2,1,0:T(8,128)S(1)} fusion(f32[16,8,128]{2,1,0:T(8,128)S(1)} %dynamic-slice_bitcast_fusion.4, s32[16,8,128]{2,1,0:T(8,128)S(1)} %dynamic-slice_bitcast_fusion.5), kind=kLoop, calls=%fused_computation.16.clone.1 | loop fusion | flops 12058624 | bytes 2228224 | tf_op jit(solution)/shard_map/while/body/eval_jaxpr/reduce_sum | solution.py:51
  111.1 5.7 %select_reduce_fusion.4 = f32[16,128,256]{2,1,0:T(8,128)S(1)} fusion(f32[16,8,128]{2,1,0:T(8,128)S(1)} %dynamic-slice_bitcast_fusion.4, s32[16,8,128]{2,1,0:T(8,128)S(1)} %dynamic-slice_bitcast_fusion.5), kind=kLoop, calls=%fused_computation.16.clone.1 | loop fusion | flops 12058624 | bytes 2228224 | tf_op jit(solution)/shard_map/while/body/eval_jaxpr/reduce_sum | solution.py:51
  118.3 5.7 %select_reduce_fusion.4 = f32[16,128,256]{2,1,0:T(8,128)S(1)} fusion(f32[16,8,128]{2,1,0:T(8,128)S(1)} %dynamic-slice_bitcast_fusion.4, s32[16,8,128]{2,1,0:T(8,128)S(1)} %dynamic-slice_bitcast_fusion.5), kind=kLoop, calls=%fused_computation.16.clone.1 | loop fusion | flops 12058624 | bytes 2228224 | tf_op jit(solution)/shard_map/while/body/eval_jaxpr/reduce_sum | solution.py:51
  124.0 1.5 bitcast_dynamic-update-slice_fusion.2
  125.5 5.7 %select_reduce_fusion.4 = f32[16,128,256]{2,1,0:T(8,128)S(1)} fusion(f32[16,8,128]{2,1,0:T(8,128)S(1)} %dynamic-slice_bitcast_fusion.4, s32[16,8,128]{2,1,0:T(8,128)S(1)} %dynamic-slice_bitcast_fusion.5), kind=kLoop, calls=%fused_computation.16.clone.1 | loop fusion | flops 12058624 | bytes 2228224 | tf_op jit(solution)/shard_map/while/body/eval_jaxpr/reduce_sum | solution.py:51
  131.2 1.6 bitcast_dynamic-update-slice_fusion.2
  132.8 5.7 %select_reduce_fusion.4 = f32[16,128,256]{2,1,0:T(8,128)S(1)} fusion(f32[16,8,128]{2,1,0:T(8,128)S(1)} %dynamic-slice_bitcast_fusion.4, s32[16,8,128]{2,1,0:T(8,128)S(1)} %dynamic-slice_bitcast_fusion.5), kind=kLoop, calls=%fused_computation.16.clone.1 | loop fusion | flops 12058624 | bytes 2228224 | tf_op jit(solution)/shard_map/while/body/eval_jaxpr/reduce_sum | solution.py:51
  140.0 5.7 %select_reduce_fusion.4 = f32[16,128,256]{2,1,0:T(8,128)S(1)} fusion(f32[16,8,128]{2,1,0:T(8,128)S(1)} %dynamic-slice_bitcast_fusion.4, s32[16,8,128]{2,1,0:T(8,128)S(1)} %dynamic-slice_bitcast_fusion.5), kind=kLoop, calls=%fused_computation.16.clone.1 | loop fusion | flops 12058624 | bytes 2228224 | tf_op jit(solution)/shard_map/while/body/eval_jaxpr/reduce_sum | solution.py:51
  145.6 1.6 bitcast_dynamic-update-slice_fusion.2
  147.2 5.7 %select_reduce_fusion.4 = f32[16,128,256]{2,1,0:T(8,128)S(1)} fusion(f32[16,8,128]{2,1,0:T(8,128)S(1)} %dynamic-slice_bitcast_fusion.4, s32[16,8,128]{2,1,0:T(8,128)S(1)} %dynamic-slice_bitcast_fusion.5), kind=kLoop, calls=%fused_computation.16.clone.1 | loop fusion | flops 12058624 | bytes 2228224 | tf_op jit(solution)/shard_map/while/body/eval_jaxpr/reduce_sum | solution.py:51
  154.4 8.0 %multiply_reduce_fusion.2 = f32[8,16,128]{2,1,0:T(8,128)S(1)} fusion(f32[8,16,128,256]{3,2,1,0:T(8,128)} %get-tuple-element.32, f32[8,16,256]{2,1,0:T(8,128)S(1)} %bitcast.81), kind=kLoop, calls=%fused_computation.22 | loop fusion | flops 8372224 | bytes 16973824 | tf_op jit(solution)/shard_map/reduce_sum | solution.py:103
  163.1 3.6 %all-to-all-start.3 = ((f32[4,128,128]{2,1,0:T(8,128)}), f32[4,128,128]{2,1,0:T(8,128)S(1)}, u32[]{:S(2)}, u32[]{:S(2)}) async-start(f32[4,128,128]{2,1,0:T(8,128)} %broadcast_in_dim.205), calls=%async_computation.4 | async-start | bytes 524288 | tf_op jit(solution)/shard_map/all_to_all | solution.py:13
  168.0 4.7 %all-to-all-done.3 = f32[4,128,128]{2,1,0:T(8,128)S(1)} async-done(((f32[4,128,128]{2,1,0:T(8,128)}), f32[4,128,128]{2,1,0:T(8,128)S(1)}, u32[]{:S(2)}, u32[]{:S(2)}) %all-to-all-start.3) | async-done | bytes 262176 | tf_op jit(solution)/shard_map/all_to_all | solution.py:13
  173.7 8.0 %multiply_reduce_fusion.1 = f32[8,16,128]{2,1,0:T(8,128)S(1)} fusion(f32[8,16,128,256]{3,2,1,0:T(8,128)} %get-tuple-element.32, f32[8,16,256]{2,1,0:T(8,128)S(1)} %pad_maximum_fusion.2), kind=kLoop, calls=%fused_computation.21 | loop fusion | flops 8372224 | bytes 16973824 | tf_op jit(solution)/shard_map/reduce_sum | solution.py:103
  182.4 3.4 %all-to-all-start.4 = ((f32[4,128,128]{2,1,0:T(8,128)}), f32[4,128,128]{2,1,0:T(8,128)S(1)}, u32[]{:S(2)}, u32[]{:S(2)}) async-start(f32[4,128,128]{2,1,0:T(8,128)} %broadcast_in_dim.208), calls=%async_computation.5 | async-start | bytes 524288 | tf_op jit(solution)/shard_map/all_to_all | solution.py:13
  185.8 5.5 %all-to-all-done.4 = f32[4,128,128]{2,1,0:T(8,128)S(1)} async-done(((f32[4,128,128]{2,1,0:T(8,128)}), f32[4,128,128]{2,1,0:T(8,128)S(1)}, u32[]{:S(2)}, u32[]{:S(2)}) %all-to-all-start.4) | async-done | bytes 262176 | tf_op jit(solution)/shard_map/all_to_all | solution.py:13
  192.2 8.0 %multiply_reduce_fusion = f32[8,16,128]{2,1,0:T(8,128)S(1)} fusion(f32[8,16,128,256]{3,2,1,0:T(8,128)} %get-tuple-element.32, f32[8,16,256]{2,1,0:T(8,128)S(1)} %pad_maximum_fusion.3), kind=kLoop, calls=%fused_computation.20 | loop fusion | flops 8372224 | bytes 16973824 | tf_op jit(solution)/shard_map/reduce_sum | solution.py:103
  200.9 3.4 %all-to-all-start.5 = ((f32[4,128,128]{2,1,0:T(8,128)}), f32[4,128,128]{2,1,0:T(8,128)S(1)}, u32[]{:S(2)}, u32[]{:S(2)}) async-start(f32[4,128,128]{2,1,0:T(8,128)} %broadcast_in_dim.209), calls=%async_computation.6 | async-start | bytes 524288 | tf_op jit(solution)/shard_map/all_to_all | solution.py:13
  204.5 5.3 %all-to-all-done.5 = f32[4,128,128]{2,1,0:T(8,128)S(1)} async-done(((f32[4,128,128]{2,1,0:T(8,128)}), f32[4,128,128]{2,1,0:T(8,128)S(1)}, u32[]{:S(2)}, u32[]{:S(2)}) %all-to-all-start.5) | async-done | bytes 262176 | tf_op jit(solution)/shard_map/all_to_all | solution.py:13
  211.3 9.3 %all-to-all-start.6 = ((f32[64,2,128]{2,1,0:T(2,128)}), f32[64,2,128]{2,1,0:T(2,128)S(1)}, u32[]{:S(2)}, u32[]{:S(2)}) async-start(f32[64,2,128]{2,1,0:T(2,128)} %broadcast_select_fusion.2), calls=%async_computation.7 | async-start | bytes 131072 | tf_op jit(solution)/shard_map/all_to_all | solution.py:107
  220.7 9.7 %all-to-all-done.6 = f32[64,2,128]{2,1,0:T(2,128)S(1)} async-done(((f32[64,2,128]{2,1,0:T(2,128)}), f32[64,2,128]{2,1,0:T(2,128)S(1)}, u32[]{:S(2)}, u32[]{:S(2)}) %all-to-all-start.6) | async-done | bytes 65568 | tf_op jit(solution)/shard_map/all_to_all | solution.py:107
  (115 shorter events, 34.8 us)
Async XLA Ops:
  6.5 1.8 copy-start
  6.5 59.7 %reduce-scatter.2.cloned.1.call-start = ((), (), s32[]{:S(2)}) async-start(), calls=%async_computation.8 | async-start | bytes 2621440 | tf_op jit(solution)/shard_map/reduce_scatter | solution.py:82
  7.5 0.9 copy-start.6
  14.8 11.9 %all-to-all-start.1 = ((f32[4,1,32768]{2,1,0:T(1,128)}), f32[4,1,32768]{2,1,0:T(1,128)}, u32[]{:S(2)}, u32[]{:S(2)}) async-start(f32[4,1,32768]{2,1,0:T(1,128)} %broadcast_in_dim.197), calls=%async_computation.2 | async-start | bytes 1048576 | tf_op jit(solution)/shard_map/all_to_all | solution.py:13
  26.7 37.1 %all-to-all-start = ((s32[64,2,1025]{2,1,0:T(2,128)}), s32[64,2,1025]{2,1,0:T(2,128)S(1)}, u32[]{:S(2)}, u32[]{:S(2)}) async-start(s32[64,2,1025]{2,1,0:T(2,128)} %pad_add_fusion), calls=%async_computation | async-start | bytes 1179648 | tf_op jit(solution)/shard_map/all_to_all | solution.py:34
  64.2 14.2 %copy-start.1 = (s32[128,1]{0,1:T(1,128)}, s32[128,1]{0,1:T(1,128)S(1)}, u32[]{:S(2)}) copy-start(s32[128,1]{0,1:T(1,128)S(1)} %copy.17) | copy-start | bytes 1540
  68.6 26.4 %all-to-all-start.2 = ((f32[64,2,1280]{2,1,0:T(2,128)}), f32[64,2,1280]{2,1,0:T(2,128)S(1)}, u32[]{:S(2)}, u32[]{:S(2)}) async-start(f32[64,2,1280]{2,1,0:T(2,128)} %pad_maximum_fusion), calls=%async_computation.3 | async-start | bytes 1310720 | tf_op jit(solution)/shard_map/all_to_all | solution.py:34
  75.9 0.5 copy-start.3
  154.4 31.4 %copy-start.4 = (s32[128]{0:T(128)S(1)}, s32[128]{0:T(128)}, u32[]{:S(2)}) copy-start(s32[128]{0:T(128)} %copy-done.3) | copy-start | bytes 1540
  163.1 9.6 %all-to-all-start.3 = ((f32[4,128,128]{2,1,0:T(8,128)}), f32[4,128,128]{2,1,0:T(8,128)S(1)}, u32[]{:S(2)}, u32[]{:S(2)}) async-start(f32[4,128,128]{2,1,0:T(8,128)} %broadcast_in_dim.205), calls=%async_computation.4 | async-start | bytes 524288 | tf_op jit(solution)/shard_map/all_to_all | solution.py:13
  173.6 30.7 %copy-start.2 = (s32[128,1]{0,1:T(1,128)S(1)}, s32[128,1]{0,1:T(1,128)}, u32[]{:S(2)}) copy-start(s32[128,1]{0,1:T(1,128)} %copy-done.1) | copy-start | bytes 1540
  173.6 47.0 %copy-start.5 = (s32[64,1]{0,1:T(1,128)S(1)}, s32[64,1]{0,1:T(1,128)}, u32[]{:S(2)}) copy-start(s32[64,1]{0,1:T(1,128)} %param.14) | copy-start | bytes 772
  173.7 47.0 %copy-start.7 = (s32[64]{0:T(128)S(1)}, s32[64]{0:T(128)}, u32[]{:S(2)}) copy-start(s32[64]{0:T(128)} %copy-done.6) | copy-start | bytes 772
  182.4 8.9 %all-to-all-start.4 = ((f32[4,128,128]{2,1,0:T(8,128)}), f32[4,128,128]{2,1,0:T(8,128)S(1)}, u32[]{:S(2)}, u32[]{:S(2)}) async-start(f32[4,128,128]{2,1,0:T(8,128)} %broadcast_in_dim.208), calls=%async_computation.5 | async-start | bytes 524288 | tf_op jit(solution)/shard_map/all_to_all | solution.py:13
  200.9 8.9 %all-to-all-start.5 = ((f32[4,128,128]{2,1,0:T(8,128)}), f32[4,128,128]{2,1,0:T(8,128)S(1)}, u32[]{:S(2)}, u32[]{:S(2)}) async-start(f32[4,128,128]{2,1,0:T(8,128)} %broadcast_in_dim.209), calls=%async_computation.6 | async-start | bytes 524288 | tf_op jit(solution)/shard_map/all_to_all | solution.py:13
  211.3 19.1 %all-to-all-start.6 = ((f32[64,2,128]{2,1,0:T(2,128)}), f32[64,2,128]{2,1,0:T(2,128)S(1)}, u32[]{:S(2)}, u32[]{:S(2)}) async-start(f32[64,2,128]{2,1,0:T(2,128)} %broadcast_select_fusion.2), calls=%async_computation.7 | async-start | bytes 131072 | tf_op jit(solution)/shard_map/all_to_all | solution.py:107
Sparse Core Ops, SparseCore 0:
  10.9 36.8 reduce-scatter.1
where the time goes:
time: 240 us; the launch traced here: 238 us
  other arithmetic  81 us (34%)
  waiting for transfers between devices  59 us (25%)
  starting transfers between devices  49.2 us (20%)
  local copies, waits for them, and re-layouts  34.2 us (14%)
  between operations  15 us (6%)
    reduce_sum x8, other arithmetic, build(): return jnp.sum(picked, axis=1)  45.3 us
    all_to_all x2, waiting for transfers between devices, in_one_piece(): lax.all_to_all(both, axis, split_axis=split_dim, concat_axis=concat_dim,...  33.5 us
    all_to_all x2, starting transfers between devices, in_one_piece(): lax.all_to_all(both, axis, split_axis=split_dim, concat_axis=concat_dim,...  24.6 us
    reduce_sum x3, other arithmetic, on_device(): partial_sum = jnp.sum(dense * nearby[:, None, :], axis=2)  24 us
    all_to_all x4, waiting for transfers between devices, copy_for_each(): return lax.all_to_all(copies, axis, split_axis=0, concat_axis=0, tiled=True)  15.7 us
    all_to_all x4, starting transfers between devices, copy_for_each(): return lax.all_to_all(copies, axis, split_axis=0, concat_axis=0, tiled=True)  15.2 us
    dynamic_update_slice x8, local copies, waits for them, and re-layouts, tile_matrix(): dense = lax.map(build, (grouped_vals, grouped_lanes))  12.3 us
    all_to_all x1, waiting for transfers between devices, on_device(): lax.all_to_all(in_slots, 'blk', split_axis=0, concat_axis=0, tiled=True)  9.73 us
  transfers between devices with their start and end apart: 8, of which 7 were waited for; matrix products, arithmetic and copies ran while one was open for 7% of the time, Pallas kernels for 0%

commit v1 on v0

v1 whole, which is shorter than its diff:
```python
import functools

import jax
import jax.numpy as jnp
from jax import lax
from jax.experimental import pallas as pl
from jax.experimental.pallas import tpu as pltpu
from jax.sharding import PartitionSpec as P

SWEEPS = 3
EXACT = lax.Precision.HIGHEST


def pick(selector, table):
    return jnp.dot(selector, table, precision=EXACT, preferred_element_type=jnp.float32)


def iota(shape, dim):
    return lax.broadcasted_iota(jnp.int32, shape, dim)


def turned(row, size):
    square = jnp.where(iota((size, size), 0) == iota((size, size), 1), row, 0.0)
    return jnp.sum(square, axis=1, keepdims=True)


def source_slots(owner_row, tiles, slots):
    owner_col = turned(owner_row, tiles)
    same = owner_col == owner_row
    row_at, col_at = iota((tiles, tiles), 0), iota((tiles, tiles), 1)
    before_col = jnp.sum(jnp.where(same & (col_at < row_at), 1.0, 0.0), axis=1, keepdims=True)
    before_row = jnp.sum(jnp.where(same & (row_at < col_at), 1.0, 0.0), axis=0, keepdims=True)
    slot_col = 2.0 * owner_col + before_col
    slot_row = 2.0 * owner_row + before_row
    to_slots = jnp.where(iota((slots, tiles), 0).astype(jnp.float32) == slot_row, 1.0, 0.0)
    from_slots = jnp.where(iota((tiles, slots), 1).astype(jnp.float32) == slot_col, 1.0, 0.0)
    return to_slots, from_slots


def successor(owners, keys, me, tiles, key_count):
    peers, width = owners.shape
    slots = 2 * peers
    lane = iota((peers, width), 1).astype(jnp.float32)
    mine = (owners == me.astype(jnp.float32)) & (lane < tiles)
    first = jnp.min(jnp.where(mine, lane, 1e6), axis=1, keepdims=True)
    last = jnp.max(jnp.where(mine, lane, -1.0), axis=1, keepdims=True)
    key_first = jnp.sum(jnp.where(mine & (lane == first), keys, 0.0), axis=1, keepdims=True)
    key_last = jnp.sum(jnp.where(mine & (lane == last), keys, 0.0), axis=1, keepdims=True)
    key_first = jnp.where(last >= 0.0, key_first, -1.0)
    key_last = jnp.where(last > first, key_last, -1.0)
    slot = iota((peers, slots), 1)
    chosen = jnp.where(slot % 2 == 1, key_last, key_first)
    key_row = jnp.sum(jnp.where(slot // 2 == iota((peers, slots), 0), chosen, 0.0), axis=0, keepdims=True)
    ahead = key_row - turned(key_row, slots) - 1.0
    ahead = jnp.where(ahead < 0.0, ahead + key_count, ahead)
    ahead = jnp.where(key_row >= 0.0, ahead, 4.0 * key_count)
    nearest = jnp.min(ahead, axis=1, keepdims=True)
    return jnp.where(ahead == nearest, 1.0, 0.0)


def kernel(
    n_src, n_blk, tiles, stored, rows, key_count,
    vals_in, cols_in, diag_in, rhs_in, map_in, dest_in, keys_in, out,
    vals, cols, diag, rhs, owner_map, dest, keys,
    meta_own, meta_all, shares, slot_out, slot_in, next_out, next_in, prods,
    here, there, fixed, load_sem, meta_sem, share_sem, slot_sem, next_sem, prod_sem,
):
    src, blk = lax.axis_index("src"), lax.axis_index("blk")
    slots = 2 * n_blk

    barrier = pltpu.get_barrier_semaphore()

    @pl.loop(1, n_blk)
    def _(step):
        pl.semaphore_signal(barrier, 1, device_id={"blk": lax.rem(blk + step, n_blk)})

    for step in range(1, n_src):
        pl.semaphore_signal(barrier, 1, device_id={"src": lax.rem(src + step, n_src)})

    loads = [
        pltpu.make_async_copy(a, b, load_sem.at[k])
        for k, (a, b) in enumerate((
            (dest_in, dest), (keys_in, keys), (map_in, owner_map), (rhs_in.at[0], rhs),
            (diag_in.at[0], diag), (cols_in, cols), (vals_in.at[0], vals)))
    ]
    for load in loads:
        load.start()
    loads[0].wait()
    loads[1].wait()
    meta_own[...] = jnp.zeros_like(meta_own)
    meta_own[0:1, 0:tiles] = dest[...]
    meta_own[1:2, 0:tiles] = keys[...]
    meta_all[blk] = meta_own[...]
    to_slots, from_slots = source_slots(dest[...].astype(jnp.float32), tiles, slots)
    for load in loads[2:5]:
        load.wait()
    shares[src, 0] = jnp.where(owner_map[...] == src, rhs[...], 0.0)
    shares[src, 1] = diag[...]
    pl.semaphore_wait(barrier, n_blk - 1 + n_src - 1)

    def to_src(buffer, sem):
        copies = []
        for step in range(1, n_src):
            copies.append(pltpu.make_async_remote_copy(
                src_ref=buffer.at[src], dst_ref=buffer.at[src],
                send_sem=sem.at[0, step], recv_sem=sem.at[1, step],
                device_id={"src": lax.rem(src + step, n_src)}))
        for copy in copies:
            copy.start()
        return copies

    def to_blk(source, target, sem):
        @pl.loop(1, n_blk)
        def _(step):
            peer = lax.rem(blk + step, n_blk)
            pltpu.make_async_remote_copy(
                src_ref=source.at[peer], dst_ref=target.at[blk],
                send_sem=sem.at[0], recv_sem=sem.at[1], device_id={"blk": peer}).start()
        target[blk] = source[blk]

    def all_of(buffer, sem):
        most = buffer.at[pl.ds(0, n_blk - 1)]
        pltpu.make_async_copy(most, most, sem).wait()

    share_copies = to_src(shares, share_sem)

    @pl.loop(1, n_blk)
    def _(step):
        peer = lax.rem(blk + step, n_blk)
        pltpu.make_async_remote_copy(
            src_ref=meta_own, dst_ref=meta_all.at[blk],
            send_sem=meta_sem.at[0], recv_sem=meta_sem.at[1], device_id={"blk": peer}).start()

    for copy in share_copies:
        copy.wait()
    fixed[0] = functools.reduce(jnp.add, [shares[s, 0] for s in range(n_src)])
    fixed[1] = functools.reduce(jnp.add, [shares[s, 1] for s in range(n_src)])
    here[...] = fixed[0] / fixed[1]

    for sweep in range(1, SWEEPS):
        e = sweep - 1
        slot_out[e] = pick(to_slots, here[...]).reshape(n_blk, 2, rows)
        to_blk(slot_out.at[e], slot_in.at[e], slot_sem.at[e])
        if e == 0:
            all_of(meta_all, meta_sem.at[1])
            follow = successor(
                meta_all[:, 0, :].astype(jnp.float32), meta_all[:, 1, :].astype(jnp.float32), blk, tiles, key_count)
        all_of(slot_in.at[e], slot_sem.at[e, 1])
        next_out[e] = pick(follow, slot_in[e].reshape(slots, rows)).reshape(n_blk, 2, rows)
        to_blk(next_out.at[e], next_in.at[e], next_sem.at[e])
        all_of(next_in.at[e], next_sem.at[e, 1])
        there[...] = pick(from_slots, next_in[e].reshape(slots, rows))
        if e == 0:
            loads[5].wait()
            loads[6].wait()

        @pl.loop(0, tiles // 8)
        def _(group):
            base = group * 8
            lines = []
            for k in range(8):
                code = cols[base + k]
                lane = code & (rows - 1)
                own = jnp.broadcast_to(here[pl.ds(base + k, 1), :], (stored, rows))
                nxt = jnp.broadcast_to(there[pl.ds(base + k, 1), :], (stored, rows))
                near = jnp.where(
                    (code & rows) == 0,
                    jnp.take_along_axis(own, lane, axis=1),
                    jnp.take_along_axis(nxt, lane, axis=1))
                lines.append(jnp.sum(vals[base + k] * near, axis=0, keepdims=True))
            prods[e, src, pl.ds(pl.multiple_of(base, 8), 8), :] = jnp.concatenate(lines, axis=0)

        prod_copies = to_src(prods.at[e], prod_sem.at[e])
        for copy in prod_copies:
            copy.wait()
        total = functools.reduce(jnp.add, [prods[e, s] for s in range(n_src)])
        here[...] = (fixed[0] - total) / fixed[1]
    out[...] = here[...]

    all_of(meta_all, meta_sem.at[0])
    for e in range(SWEEPS - 1):
        all_of(slot_out.at[e], slot_sem.at[e, 0])
        all_of(next_out.at[e], next_sem.at[e, 0])


def solution(mesh):
    n_src, n_blk = mesh.shape["src"], mesh.shape["blk"]

    def on_device(values, diagonal, rhs_parts, owner_map, columns, destination, order_keys):
        tiles, stored, rows = columns.shape
        key_count = float(tiles * n_blk)
        row = jnp.float32
        anywhere = pl.BlockSpec(memory_space=pl.ANY)
        steps = SWEEPS - 1
        dma = pltpu.SemaphoreType.DMA
        return pl.pallas_call(
            functools.partial(kernel, n_src, n_blk, tiles, stored, rows, key_count),
            out_shape=jax.ShapeDtypeStruct((tiles, rows), row),
            in_specs=[anywhere] * 7,
            out_specs=pl.BlockSpec(memory_space=pltpu.VMEM),
            scratch_shapes=[
                pltpu.VMEM((tiles, stored, rows), row),
                pltpu.VMEM((tiles, stored, rows), jnp.int32),
                pltpu.VMEM((tiles, rows), row),
                pltpu.VMEM((tiles, rows), row),
                pltpu.VMEM((tiles, rows), jnp.int32),
                pltpu.VMEM((1, tiles), jnp.int32),
                pltpu.VMEM((1, tiles), jnp.int32),
                pltpu.VMEM((2, rows), jnp.int32),
                pltpu.VMEM((n_blk, 2, rows), jnp.int32),
                pltpu.VMEM((n_src, 2, tiles, rows), row),
                pltpu.VMEM((steps, n_blk, 2, rows), row),
                pltpu.VMEM((steps, n_blk, 2, rows), row),
                pltpu.VMEM((steps, n_blk, 2, rows), row),
                pltpu.VMEM((steps, n_blk, 2, rows), row),
                pltpu.VMEM((steps, n_src, tiles, rows), row),
                pltpu.VMEM((tiles, rows), row),
                pltpu.VMEM((tiles, rows), row),
                pltpu.VMEM((2, tiles, rows), row),
                dma((7,)),
                dma((2,)),
                dma((2, n_src)),
                dma((steps, 2)),
                dma((steps, 2)),
                dma((steps, 2, n_src)),
            ],
            compiler_params=pltpu.CompilerParams(collective_id=0, has_side_effects=True),
            name="sweeps",
        )(values, columns, diagonal, rhs_parts, owner_map,
          destination.reshape(1, tiles), order_keys.reshape(1, tiles))

    placed = (
        P("src", "blk", None, None), P("src", "blk", None), P("src", "blk", None),
        P("blk", None), P("blk", None, None), P("blk", None), P("blk"),
    )
    return jax.shard_map(
        on_device, mesh=mesh, in_specs=placed, out_specs=P("blk", None), check_vma=False)
```

time: 240 us -> 58.5 us (0.24)
  other arithmetic: 81 us -> 0 us
  waiting for transfers between devices: 59 us -> 0 us
  Pallas kernels: 0 us -> 57 us
  starting transfers between devices: 49.2 us -> 0 us
  local copies, waits for them, and re-layouts: 34.2 us -> 1.38 us
  between operations: 15 us -> 0.01 us
    reduce_sum x20 -> x0, other arithmetic: 72.8 us -> none  [the longest x8 45.3 us: build(): return jnp.sum(picked, axis=1)]
    all_to_all x7 -> x0, waiting for transfers between devices: 58.9 us -> none  [the longest x2 33.5 us: in_one_piece(): lax.all_to_all(both, axis, split_axis=split_dim, concat_axis=concat_dim,...]
    pallas_call x0 -> x1, Pallas kernels: none -> 57 us  [on_device(): pl.pallas_call(functools.partial(kernel, n_src, n_blk, tiles, stored, row...]
    all_to_all x7 -> x0, starting transfers between devices: 49.2 us -> none  [the longest x2 24.6 us: in_one_piece(): lax.all_to_all(both, axis, split_axis=split_dim, concat_axis=concat_dim,...]
    gather x14 -> x0, local copies, waits for them, and re-layouts: 12.9 us -> none  [the longest x3 1.94 us: on_device(): nearby = jnp.concatenate([iterate, iterate[following]], axis=1)]
    dynamic_update_slice x8 -> x0, local copies, waits for them, and re-layouts: 12.3 us -> none  [tile_matrix(): dense = lax.map(build, (grouped_vals, grouped_lanes))]
    select_n x17 -> x0, other arithmetic: 4.19 us -> none  [the longest x1 1.57 us: on_device(): send_vals = jnp.where(filled[:, None, None], values[0][source_tile], 0.0)]
    broadcast_in_dim x14 -> x0, local copies, waits for them, and re-layouts: 3.4 us -> none  [the longest x4 3.2 us: copy_for_each(): copies = jnp.broadcast_to(value, (lax.axis_size(axis), *value.shape))]
  transfers between devices with their start and end apart: 8 -> 0, of which waited for: 7 -> 0; matrix products, arithmetic and copies ran while one was open for 7% -> 0% of each run, Pallas kernels for 0% -> 0%
where the time goes in v1:
time: 58.5 us; the launch traced here: 58.4 us
  Pallas kernels  57 us (97%)
  local copies, waits for them, and re-layouts  1.38 us (2%)
    pallas_call x1, Pallas kernels, on_device(): pl.pallas_call(functools.partial(kernel, n_src, n_blk, tiles, stored, row...  57 us
    unnamed x1, local copies, waits for them, and re-layouts  1.38 us

profile of v1, /device:TPU:1, one launch (start us, length us, event | category | flops | bytes accessed | tf_op | source)
XLA Modules:
  0.0 58.4 jit_solution(10001038186817638872)
XLA Ops:
  0.0 57.0 %sweeps.1 = f32[64,128]{1,0:T(8,128)} custom-call(f32[1,64,32,128]{3,2,1,0:T(8,128)} %vals_in.1, s32[64,32,128]{2,1,0:T(8,128)} %cols_in.1, f32[1,64,128]{2,1,0:T(8,128)} %diag_in.1, f32[1,64,128]{2,1,0:T(8,128)} %rhs_in.1, s32[64,128]{1,0:T(8,128)} %map_in.1, s32[1,64]{1,0:T(1,128)} %bitcast.2, s32[1,64]{1,0:T(1,128)} %bitcast.3), custom_call_target="tpu_custom_call" | custom-call | tf_op jit(solution)/shard_map/sweeps/pallas_call | solution.py:196
  57.0 1.4 %copy.9 = f32[64,128]{1,0:T(8,128)} copy(f32[64,128]{1,0:T(8,128)} %sweeps.1) | data formatting | bytes 65536

commit v2 on v1

--- a/solution.py
+++ b/solution.py
@@ -58,15 +58,49 @@
     return jnp.where(ahead == nearest, 1.0, 0.0)
 
 
+def folded(parts):
+    parts = [parts[k] for k in (0, 4, 2, 6, 1, 5, 3, 7)]
+    line = iota(parts[0].shape, 0)
+    for step in (1, 2, 4):
+        half = len(parts) // 2
+        low = (line & step) == 0
+        parts = [
+            jnp.where(low, parts[k], parts[k + half])
+            + pltpu.roll(jnp.where(low, parts[k + half], parts[k]), step, 0)
+            for k in range(half)
+        ]
+    return parts[0]
+
+
+def products(vals, cols, lines, v0, t0, bit):
+    _, stored, rows = cols.shape
+    parts = []
+    for k in range(8):
+        line = jnp.broadcast_to(lines[pl.ds(t0 + k, 1), :], (8, rows))
+        total = None
+        for j in range(stored // 8):
+            code = cols[t0 + k, pl.ds(8 * j, 8), :]
+            near = jnp.take_along_axis(line, code & (rows - 1), axis=1, mode="promise_in_bounds")
+            term = jnp.where((code & rows) == bit, vals[v0 + k, pl.ds(8 * j, 8), :], 0.0) * near
+            total = term if total is None else total + term
+        parts.append(total)
+    return folded(parts)
+
+
 def kernel(
-    n_src, n_blk, tiles, stored, rows, key_count,
+    n_src, n_blk, grid, tiles, stored, rows, key_count,
     vals_in, cols_in, diag_in, rhs_in, map_in, dest_in, keys_in, out,
     vals, cols, diag, rhs, owner_map, dest, keys,
-    meta_own, meta_all, shares, slot_out, slot_in, next_out, next_in, prods,
-    here, there, fixed, load_sem, meta_sem, share_sem, slot_sem, next_sem, prod_sem,
+    meta_own, meta_all, shares, slot_out, slot_in, next_out, next_in,
+    parts, full, quarters, here, there, near, fixed,
+    load_sem, meta_sem, share_sem, slot_sem, next_sem, part_sem, full_sem, quarter_sem,
 ):
     src, blk = lax.axis_index("src"), lax.axis_index("blk")
     slots = 2 * n_blk
+    share = tiles // n_src
+    n_y, n_z = grid
+    y, z, core = blk // (2 * n_z), (blk // 2) % n_z, blk % 2
+    src_steps = sorted(range(1, n_src), key=lambda step: -min(step, n_src - step))
 
     barrier = pltpu.get_barrier_semaphore()
 
@@ -74,14 +108,16 @@
     def _(step):
         pl.semaphore_signal(barrier, 1, device_id={"blk": lax.rem(blk + step, n_blk)})
 
-    for step in range(1, n_src):
+    for step in src_steps:
         pl.semaphore_signal(barrier, 1, device_id={"src": lax.rem(src + step, n_src)})
 
+    mine = pl.ds(pl.multiple_of(src * share, share), share)
     loads = [
         pltpu.make_async_copy(a, b, load_sem.at[k])
         for k, (a, b) in enumerate((
             (dest_in, dest), (keys_in, keys), (map_in, owner_map), (rhs_in.at[0], rhs),
-            (diag_in.at[0], diag), (cols_in, cols), (vals_in.at[0], vals)))
+            (diag_in.at[0], diag), (vals_in.at[0], vals), (vals_in.at[0, mine], parts.at[src]),
+            (cols_in, cols)))
     ]
     for load in loads:
         load.start()
@@ -96,86 +132,108 @@
         load.wait()
     shares[src, 0] = jnp.where(owner_map[...] == src, rhs[...], 0.0)
     shares[src, 1] = diag[...]
+    for load in loads[5:]:
+        load.wait()
     pl.semaphore_wait(barrier, n_blk - 1 + n_src - 1)
 
-    def to_src(buffer, sem):
+    def to_src(source, target, sem):
         copies = []
-        for step in range(1, n_src):
+        for step in src_steps:
+            peer = lax.rem(src + step, n_src)
             copies.append(pltpu.make_async_remote_copy(
-                src_ref=buffer.at[src], dst_ref=buffer.at[src],
-                send_sem=sem.at[0, step], recv_sem=sem.at[1, step],
-                device_id={"src": lax.rem(src + step, n_src)}))
+                src_ref=source(peer), dst_ref=target, send_sem=sem.at[0, step],
+                recv_sem=sem.at[1, step], device_id={"src": peer}))
         for copy in copies:
             copy.start()
         return copies
 
     def to_blk(source, target, sem):
-        @pl.loop(1, n_blk)
+        @pl.loop(0, n_blk - 1)
         def _(step):
-            peer = lax.rem(blk + step, n_blk)
+            turn_z, turn_y, turn_c = step // (2 * n_y), (step // 2) % n_y, step % 2
+            to_z = n_z // 2 + (turn_z % 2) * -(turn_z // 2 + 1) + (1 - turn_z % 2) * (turn_z // 2)
+            to_y = n_y // 2 + (turn_y % 2) * -(turn_y // 2 + 1) + (1 - turn_y % 2) * (turn_y // 2)
+            peer = (((y + to_y) % n_y) * n_z + (z + to_z) % n_z) * 2 + (core + 1 + turn_c) % 2
             pltpu.make_async_remote_copy(
-                src_ref=source.at[peer], dst_ref=target.at[blk],
+                src_ref=source(peer), dst_ref=target.at[blk],
                 send_sem=sem.at[0], recv_sem=sem.at[1], device_id={"blk": peer}).start()
-        target[blk] = source[blk]
 
     def all_of(buffer, sem):
         most = buffer.at[pl.ds(0, n_blk - 1)]
         pltpu.make_async_copy(most, most, sem).wait()
 
-    share_copies = to_src(shares, share_sem)
-
-    @pl.loop(1, n_blk)
-    def _(step):
-        peer = lax.rem(blk + step, n_blk)
-        pltpu.make_async_remote_copy(
-            src_ref=meta_own, dst_ref=meta_all.at[blk],
-            send_sem=meta_sem.at[0], recv_sem=meta_sem.at[1], device_id={"blk": peer}).start()
-
+    def through_owners(e, lines, follow):
+        slot_out[e] = pick(to_slots, lines).reshape(n_blk, 2, rows)
+        to_blk(lambda peer: slot_out.at[e, peer], slot_in.at[e], slot_sem.at[e])
+        slot_in[e, blk] = slot_out[e, blk]
+        if follow is None:
+            all_of(meta_all, meta_sem.at[1])
+            follow = successor(
+                meta_all[:, 0, :].astype(jnp.float32), meta_all[:, 1, :].astype(jnp.float32),
+                blk, tiles, key_count)
+        all_of(slot_in.at[e], slot_sem.at[e, 1])
+        next_out[e] = pick(follow, slot_in[e].reshape(slots, rows)).reshape(n_blk, 2, rows)
+        to_blk(lambda peer: next_out.at[e, peer], next_in.at[e], next_sem.at[e])
+        next_in[e, blk] = next_out[e, blk]
+        return follow
+
+    def from_owners(e):
+        all_of(next_in.at[e], next_sem.at[e, 1])
+        there[...] = pick(from_slots, next_in[e].reshape(slots, rows))
+
+    share_copies = to_src(lambda peer: shares.at[src], shares.at[src], share_sem)
+    to_blk(lambda peer: meta_own, meta_all, meta_sem)
+    part_copies = to_src(
+        lambda peer: vals.at[pl.ds(pl.multiple_of(peer * share, share), share)], parts.at[src], part_sem)
     for copy in share_copies:
         copy.wait()
     fixed[0] = functools.reduce(jnp.add, [shares[s, 0] for s in range(n_src)])
     fixed[1] = functools.reduce(jnp.add, [shares[s, 1] for s in range(n_src)])
     here[...] = fixed[0] / fixed[1]
-
-    for sweep in range(1, SWEEPS):
-        e = sweep - 1
-        slot_out[e] = pick(to_slots, here[...]).reshape(n_blk, 2, rows)
-        to_blk(slot_out.at[e], slot_in.at[e], slot_sem.at[e])
-        if e == 0:
-            all_of(meta_all, meta_sem.at[1])
-            follow = successor(
-                meta_all[:, 0, :].astype(jnp.float32), meta_all[:, 1, :].astype(jnp.float32), blk, tiles, key_count)
-        all_of(slot_in.at[e], slot_sem.at[e, 1])
-        next_out[e] = pick(follow, slot_in[e].reshape(slots, rows)).reshape(n_blk, 2, rows)
-        to_blk(next_out.at[e], next_in.at[e], next_sem.at[e])
-        all_of(next_in.at[e], next_sem.at[e, 1])
-        there[...] = pick(from_slots, next_in[e].reshape(slots, rows))
-        if e == 0:
-            loads[5].wait()
-            loads[6].wait()
-
-        @pl.loop(0, tiles // 8)
-        def _(group):
-            base = group * 8
-            lines = []
-            for k in range(8):
-                code = cols[base + k]
-                lane = code & (rows - 1)
-                own = jnp.broadcast_to(here[pl.ds(base + k, 1), :], (stored, rows))
-                nxt = jnp.broadcast_to(there[pl.ds(base + k, 1), :], (stored, rows))
-                near = jnp.where(
-                    (code & rows) == 0,
-                    jnp.take_along_axis(own, lane, axis=1),
-                    jnp.take_along_axis(nxt, lane, axis=1))
-                lines.append(jnp.sum(vals[base + k] * near, axis=0, keepdims=True))
-            prods[e, src, pl.ds(pl.multiple_of(base, 8), 8), :] = jnp.concatenate(lines, axis=0)
-
-        prod_copies = to_src(prods.at[e], prod_sem.at[e])
-        for copy in prod_copies:
-            copy.wait()
-        total = functools.reduce(jnp.add, [prods[e, s] for s in range(n_src)])
-        here[...] = (fixed[0] - total) / fixed[1]
-    out[...] = here[...]
+    follow = through_owners(0, here[...], None)
+
+    for copy in part_copies:
+        copy.wait()
+
+    @pl.loop(0, share)
+    def _(k):
+        full[src, k] = functools.reduce(jnp.add, [parts[s, k] for s in range(n_src)])
+
+    first = pl.multiple_of(src * share, share)
+
+    @pl.loop(0, share // 8)
+    def _(g):
+        near[pl.ds(pl.multiple_of(first + g * 8, 8), 8), :] = products(
+            full.at[src], cols, here, g * 8, first + g * 8, 0)
+
+    from_owners(0)
+    for g in range(share // 8):
+        at = pl.ds(pl.multiple_of(first + g * 8, 8), 8)
+        total = near[at, :] + products(full.at[src], cols, there, g * 8, first + g * 8, rows)
+        quarters[src, pl.ds(g * 8, 8), :] = (fixed[0, at, :] - total) / fixed[1, at, :]
+    quarter_copies = to_src(lambda peer: quarters.at[src], quarters.at[src], quarter_sem)
+    full_copies = to_src(lambda peer: full.at[src], full.at[src], full_sem)
+    for copy in quarter_copies:
+        copy.wait()
+    here[...] = quarters[...].reshape(tiles, rows)
+    through_owners(1, here[...], follow)
+
+    def near_of(s):
+        @pl.loop(0, share // 8)
+        def _(g):
+            start = s * share + g * 8
+            near[pl.ds(pl.multiple_of(start, 8), 8), :] = products(full.at[s], cols, here, g * 8, start, 0)
+
+    near_of(src)
+    for step, copy in sorted(zip(src_steps, full_copies), key=lambda pair: min(pair[0], n_src - pair[0])):
+        copy.wait()
+        near_of(lax.rem(src - step + n_src, n_src))
+    from_owners(1)
+    for s in range(n_src):
+        for g in range(share // 8):
+            at = pl.ds(s * share + g * 8, 8)
+            total = near[at, :] + products(full.at[s], cols, there, g * 8, s * share + g * 8, rows)
+            out[at, :] = (fixed[0, at, :] - total) / fixed[1, at, :]
 
     all_of(meta_all, meta_sem.at[0])
     for e in range(SWEEPS - 1):
@@ -185,6 +243,7 @@
 
 def solution(mesh):
     n_src, n_blk = mesh.shape["src"], mesh.shape["blk"]
+    grid = (4, n_blk // 8)
 
     def on_device(values, diagonal, rhs_parts, owner_map, columns, destination, order_keys):
         tiles, stored, rows = columns.shape
@@ -194,7 +253,7 @@
         steps = SWEEPS - 1
         dma = pltpu.SemaphoreType.DMA
         return pl.pallas_call(
-            functools.partial(kernel, n_src, n_blk, tiles, stored, rows, key_count),
+            functools.partial(kernel, n_src, n_blk, grid, tiles, stored, rows, key_count),
             out_shape=jax.ShapeDtypeStruct((tiles, rows), row),
             in_specs=[anywhere] * 7,
             out_specs=pl.BlockSpec(memory_space=pltpu.VMEM),
@@ -213,16 +272,21 @@
                 pltpu.VMEM((steps, n_blk, 2, rows), row),
                 pltpu.VMEM((steps, n_blk, 2, rows), row),
                 pltpu.VMEM((steps, n_blk, 2, rows), row),
-                pltpu.VMEM((steps, n_src, tiles, rows), row),
+                pltpu.VMEM((n_src, tiles // n_src, stored, rows), row),
+                pltpu.VMEM((n_src, tiles // n_src, stored, rows), row),
+                pltpu.VMEM((n_src, tiles // n_src, rows), row),
+                pltpu.VMEM((tiles, rows), row),
                 pltpu.VMEM((tiles, rows), row),
                 pltpu.VMEM((tiles, rows), row),
                 pltpu.VMEM((2, tiles, rows), row),
-                dma((7,)),
+                dma((8,)),
                 dma((2,)),
                 dma((2, n_src)),
                 dma((steps, 2)),
                 dma((steps, 2)),
-                dma((steps, 2, n_src)),
+                dma((2, n_src)),
+                dma((2, n_src)),
+                dma((2, n_src)),
             ],
             compiler_params=pltpu.CompilerParams(collective_id=0, has_side_effects=True),
             name="sweeps",

time: 58.5 us -> 58.7 us (level)
  no operation moved by 1% of the time
where the time goes in v2:
time: 58.7 us; the launch traced here: 58.5 us
  Pallas kernels  57.1 us (97%)
  local copies, waits for them, and re-layouts  1.38 us (2%)
    pallas_call x1, Pallas kernels, on_device(): pl.pallas_call(functools.partial(kernel, n_src, n_blk, grid, tiles, store...  57.1 us
    unnamed x1, local copies, waits for them, and re-layouts  1.38 us

profile of v2, /device:TPU:1, one launch (start us, length us, event | category | flops | bytes accessed | tf_op | source)
XLA Modules:
  0.0 58.5 jit_solution(11748797203663036456)
XLA Ops:
  0.0 57.1 %sweeps.1 = f32[64,128]{1,0:T(8,128)} custom-call(f32[1,64,32,128]{3,2,1,0:T(8,128)} %vals_in.1, s32[64,32,128]{2,1,0:T(8,128)} %cols_in.1, f32[1,64,128]{2,1,0:T(8,128)} %diag_in.1, f32[1,64,128]{2,1,0:T(8,128)} %rhs_in.1, s32[64,128]{1,0:T(8,128)} %map_in.1, s32[1,64]{1,0:T(1,128)} %bitcast.2, s32[1,64]{1,0:T(1,128)} %bitcast.3), custom_call_target="tpu_custom_call" | custom-call | tf_op jit(solution)/shard_map/sweeps/pallas_call | solution.py:255
  57.1 1.4 %copy.9 = f32[64,128]{1,0:T(8,128)} copy(f32[64,128]{1,0:T(8,128)} %sweeps.1) | data formatting | bytes 65536

commit v3 on v2

--- a/solution.py
+++ b/solution.py
@@ -93,7 +93,7 @@
     vals, cols, diag, rhs, owner_map, dest, keys,
     meta_own, meta_all, shares, slot_out, slot_in, next_out, next_in,
     parts, full, quarters, here, there, near, fixed,
-    load_sem, meta_sem, share_sem, slot_sem, next_sem, part_sem, full_sem, quarter_sem,
+    load_sem, meta_sem, share_sem, slot_sem, next_sem, part_sem, full_sem, quarter_sem, group_sem, open_sem,
 ):
     src, blk = lax.axis_index("src"), lax.axis_index("blk")
     slots = 2 * n_blk
@@ -102,14 +102,20 @@
     y, z, core = blk // (2 * n_z), (blk // 2) % n_z, blk % 2
     src_steps = sorted(range(1, n_src), key=lambda step: -min(step, n_src - step))
 
+    def far_first(step):
+        turn_z, turn_y, turn_c = step // (2 * n_y), (step // 2) % n_y, step % 2
+        to_z = n_z // 2 + (turn_z % 2) * -(turn_z // 2 + 1) + (1 - turn_z % 2) * (turn_z // 2)
+        to_y = n_y // 2 + (turn_y % 2) * -(turn_y // 2 + 1) + (1 - turn_y % 2) * (turn_y // 2)
+        return (((y + to_y) % n_y) * n_z + (z + to_z) % n_z) * 2 + (core + 1 + turn_c) % 2
+
     barrier = pltpu.get_barrier_semaphore()
-
-    @pl.loop(1, n_blk)
-    def _(step):
-        pl.semaphore_signal(barrier, 1, device_id={"blk": lax.rem(blk + step, n_blk)})
-
+    leader = n_src - 1
     for step in src_steps:
-        pl.semaphore_signal(barrier, 1, device_id={"src": lax.rem(src + step, n_src)})
+        peer = lax.rem(src + step, n_src)
+
+        @pl.when(peer != leader)
+        def _():
+            pl.semaphore_signal(barrier, 1, device_id={"src": peer})
 
     mine = pl.ds(pl.multiple_of(src * share, share), share)
     loads = [
@@ -134,7 +140,19 @@
     shares[src, 1] = diag[...]
     for load in loads[5:]:
         load.wait()
-    pl.semaphore_wait(barrier, n_blk - 1 + n_src - 1)
+
+    @pl.when(src != leader)
+    def _():
+        pl.semaphore_wait(barrier, n_src - 1)
+        pl.semaphore_signal(group_sem, 1, device_id={"src": leader})
+
+    @pl.when(src == leader)
+    def _():
+        pl.semaphore_wait(group_sem, n_src - 1)
+
+        @pl.loop(0, n_blk - 1)
+        def _(step):
+            pl.semaphore_signal(barrier, 1, device_id={"blk": far_first(step)})
 
     def to_src(source, target, sem):
         copies = []
@@ -150,19 +168,22 @@
     def to_blk(source, target, sem):
         @pl.loop(0, n_blk - 1)
         def _(step):
-            turn_z, turn_y, turn_c = step // (2 * n_y), (step // 2) % n_y, step % 2
-            to_z = n_z // 2 + (turn_z % 2) * -(turn_z // 2 + 1) + (1 - turn_z % 2) * (turn_z // 2)
-            to_y = n_y // 2 + (turn_y % 2) * -(turn_y // 2 + 1) + (1 - turn_y % 2) * (turn_y // 2)
-            peer = (((y + to_y) % n_y) * n_z + (z + to_z) % n_z) * 2 + (core + 1 + turn_c) % 2
+            peer = far_first(step)
             pltpu.make_async_remote_copy(
                 src_ref=source(peer), dst_ref=target.at[blk],
                 send_sem=sem.at[0], recv_sem=sem.at[1], device_id={"blk": peer}).start()
 
+    def ring_copy(chunk, part, step, k):
+        block = full.at[chunk, part] if part is not None else full.at[chunk]
+        return pltpu.make_async_remote_copy(
+            src_ref=block, dst_ref=block, send_sem=full_sem.at[0, k], recv_sem=full_sem.at[1, k],
+            device_id={"src": (src + step) % n_src})
+
     def all_of(buffer, sem):
         most = buffer.at[pl.ds(0, n_blk - 1)]
         pltpu.make_async_copy(most, most, sem).wait()
 
-    def through_owners(e, lines, follow):
+    def through_owners(e, lines, follow, meanwhile=lambda: None):
         slot_out[e] = pick(to_slots, lines).reshape(n_blk, 2, rows)
         to_blk(lambda peer: slot_out.at[e, peer], slot_in.at[e], slot_sem.at[e])
         slot_in[e, blk] = slot_out[e, blk]
@@ -171,6 +192,7 @@
             follow = successor(
                 meta_all[:, 0, :].astype(jnp.float32), meta_all[:, 1, :].astype(jnp.float32),
                 blk, tiles, key_count)
+        meanwhile()
         all_of(slot_in.at[e], slot_sem.at[e, 1])
         next_out[e] = pick(follow, slot_in[e].reshape(slots, rows)).reshape(n_blk, 2, rows)
         to_blk(lambda peer: next_out.at[e, peer], next_in.at[e], next_sem.at[e])
@@ -182,9 +204,20 @@
         there[...] = pick(from_slots, next_in[e].reshape(slots, rows))
 
     share_copies = to_src(lambda peer: shares.at[src], shares.at[src], share_sem)
-    to_blk(lambda peer: meta_own, meta_all, meta_sem)
     part_copies = to_src(
         lambda peer: vals.at[pl.ds(pl.multiple_of(peer * share, share), share)], parts.at[src], part_sem)
+
+    @pl.when(src == leader)
+    def _():
+        pl.semaphore_wait(barrier, n_blk - 1)
+        for step in src_steps:
+            pl.semaphore_signal(open_sem, 1, device_id={"src": lax.rem(src + step, n_src)})
+
+    @pl.when(src != leader)
+    def _():
+        pl.semaphore_wait(open_sem, 1)
+
+    to_blk(lambda peer: meta_own, meta_all, meta_sem)
     for copy in share_copies:
         copy.wait()
     fixed[0] = functools.reduce(jnp.add, [shares[s, 0] for s in range(n_src)])
@@ -212,11 +245,24 @@
         total = near[at, :] + products(full.at[src], cols, there, g * 8, first + g * 8, rows)
         quarters[src, pl.ds(g * 8, 8), :] = (fixed[0, at, :] - total) / fixed[1, at, :]
     quarter_copies = to_src(lambda peer: quarters.at[src], quarters.at[src], quarter_sem)
-    full_copies = to_src(lambda peer: full.at[src], full.at[src], full_sem)
+    to_right, to_left = ring_copy(src, None, 1, 0), ring_copy(src, None, -1, 1)
+    to_right.start()
+    to_left.start()
     for copy in quarter_copies:
         copy.wait()
     here[...] = quarters[...].reshape(tiles, rows)
-    through_owners(1, here[...], follow)
+
+    left, right, across = (src - 1) % n_src, (src + 1) % n_src, (src + 2) % n_src
+    halves = pl.ds(0, share // 2), pl.ds(share // 2, share // 2)
+    onward = ring_copy(left, halves[0], 1, 2), ring_copy(right, halves[1], -1, 3)
+
+    def pass_on():
+        to_right.wait()
+        onward[0].start()
+        to_left.wait()
+        onward[1].start()
+
+    through_owners(1, here[...], follow, pass_on)
 
     def near_of(s):
         @pl.loop(0, share // 8)
@@ -224,10 +270,11 @@
             start = s * share + g * 8
             near[pl.ds(pl.multiple_of(start, 8), 8), :] = products(full.at[s], cols, here, g * 8, start, 0)
 
-    near_of(src)
-    for step, copy in sorted(zip(src_steps, full_copies), key=lambda pair: min(pair[0], n_src - pair[0])):
-        copy.wait()
-        near_of(lax.rem(src - step + n_src, n_src))
+    for chunk in (src, left, right):
+        near_of(chunk)
+    onward[0].wait()
+    onward[1].wait()
+    near_of(across)
     from_owners(1)
     for s in range(n_src):
         for g in range(share // 8):
@@ -254,7 +301,7 @@
         dma = pltpu.SemaphoreType.DMA
         return pl.pallas_call(
             functools.partial(kernel, n_src, n_blk, grid, tiles, stored, rows, key_count),
-            out_shape=jax.ShapeDtypeStruct((tiles, rows), row),
+            out_shape=pltpu.VMEM((tiles, rows), row),
             in_specs=[anywhere] * 7,
             out_specs=pl.BlockSpec(memory_space=pltpu.VMEM),
             scratch_shapes=[
@@ -285,8 +332,10 @@
                 dma((steps, 2)),
                 dma((steps, 2)),
                 dma((2, n_src)),
+                dma((2, 4)),
                 dma((2, n_src)),
-                dma((2, n_src)),
+                pltpu.SemaphoreType.REGULAR,
+                pltpu.SemaphoreType.REGULAR,
             ],
             compiler_params=pltpu.CompilerParams(collective_id=0, has_side_effects=True),
             name="sweeps",

time: 58.7 us -> 51.7 us (0.88)
  Pallas kernels: 57.1 us -> 50.8 us
  local copies, waits for them, and re-layouts: 1.38 us -> 0.62 us
    pallas_call x1, Pallas kernels: 57.1 us -> 50.8 us  [on_device(): pl.pallas_call(functools.partial(kernel, n_src, n_blk, grid, tiles, store...]
    unnamed x1, local copies, waits for them, and re-layouts: 1.38 us -> 0.62 us
where the time goes in v3:
time: 51.7 us; the launch traced here: 51.4 us
  Pallas kernels  50.8 us (98%)
  local copies, waits for them, and re-layouts  0.62 us (1%)
    pallas_call x1, Pallas kernels, on_device(): pl.pallas_call(functools.partial(kernel, n_src, n_blk, grid, tiles, store...  50.8 us

profile of v3, /device:TPU:1, one launch (start us, length us, event | category | flops | bytes accessed | tf_op | source)
XLA Modules:
  0.0 51.4 jit_solution(2156830476229817188)
XLA Ops:
  0.0 50.8 %sweeps.1 = f32[64,128]{1,0:T(8,128)S(1)} custom-call(f32[1,64,32,128]{3,2,1,0:T(8,128)} %vals_in.1, s32[64,32,128]{2,1,0:T(8,128)} %cols_in.1, f32[1,64,128]{2,1,0:T(8,128)} %diag_in.1, f32[1,64,128]{2,1,0:T(8,128)} %rhs_in.1, s32[64,128]{1,0:T(8,128)} %map_in.1, s32[1,64]{1,0:T(1,128)} %bitcast.2, s32[1,64]{1,0:T(1,128)} %bitcast.3), custom_call_target="tpu_custom_call" | custom-call | tf_op jit(solution)/shard_map/sweeps/pallas_call | solution.py:302
  50.8 0.6 %copy.9 = f32[64,128]{1,0:T(8,128)} copy(f32[64,128]{1,0:T(8,128)S(1)} %sweeps.1) | data formatting | bytes 65536

commit v4 on v3

--- a/solution.py
+++ b/solution.py
@@ -92,7 +92,7 @@
     vals_in, cols_in, diag_in, rhs_in, map_in, dest_in, keys_in, out,
     vals, cols, diag, rhs, owner_map, dest, keys,
     meta_own, meta_all, shares, slot_out, slot_in, next_out, next_in,
-    parts, full, quarters, here, there, near, fixed,
+    hold, full, quarters, here, there, near, fixed,
     load_sem, meta_sem, share_sem, slot_sem, next_sem, part_sem, full_sem, quarter_sem, group_sem, open_sem,
 ):
     src, blk = lax.axis_index("src"), lax.axis_index("blk")
@@ -102,28 +102,34 @@
     y, z, core = blk // (2 * n_z), (blk // 2) % n_z, blk % 2
     src_steps = sorted(range(1, n_src), key=lambda step: -min(step, n_src - step))
 
-    def far_first(step):
-        turn_z, turn_y, turn_c = step // (2 * n_y), (step // 2) % n_y, step % 2
-        to_z = n_z // 2 + (turn_z % 2) * -(turn_z // 2 + 1) + (1 - turn_z % 2) * (turn_z // 2)
-        to_y = n_y // 2 + (turn_y % 2) * -(turn_y // 2 + 1) + (1 - turn_y % 2) * (turn_y // 2)
-        return (((y + to_y) % n_y) * n_z + (z + to_z) % n_z) * 2 + (core + 1 + turn_c) % 2
+    def by_distance(n):
+        return sorted(range(n), key=lambda d: -min(d, n - d))
+
+    at_z = {d: (z + d) % n_z * 2 for d in range(n_z)}
+    at_y = {d: (y + d) % n_y * (2 * n_z) for d in range(n_y)}
+    at_core = core, 1 - core
+    others = [
+        at_y[to_y] + at_z[to_z] + at_core[to_core]
+        for to_z in by_distance(n_z) for to_y in by_distance(n_y) for to_core in (1, 0)
+    ][:-1]
 
     barrier = pltpu.get_barrier_semaphore()
-    leader = n_src - 1
-    for step in src_steps:
-        peer = lax.rem(src + step, n_src)
-
-        @pl.when(peer != leader)
-        def _():
-            pl.semaphore_signal(barrier, 1, device_id={"src": peer})
-
-    mine = pl.ds(pl.multiple_of(src * share, share), share)
+    hub, relay = 0, 1
+
+    @pl.when(src != hub)
+    def _():
+        pl.semaphore_signal(barrier, 1, device_id={"src": hub})
+
+    plane = jnp.maximum(src, relay)
+
+    for peer in others:
+        pl.semaphore_signal(barrier, 1, device_id={"src": plane, "blk": peer})
+
     loads = [
         pltpu.make_async_copy(a, b, load_sem.at[k])
         for k, (a, b) in enumerate((
             (dest_in, dest), (keys_in, keys), (map_in, owner_map), (rhs_in.at[0], rhs),
-            (diag_in.at[0], diag), (vals_in.at[0], vals), (vals_in.at[0, mine], parts.at[src]),
-            (cols_in, cols)))
+            (diag_in.at[0], diag), (vals_in.at[0], vals), (cols_in, cols)))
     ]
     for load in loads:
         load.start()
@@ -141,18 +147,15 @@
     for load in loads[5:]:
         load.wait()
 
-    @pl.when(src != leader)
+    @pl.when(src == hub)
     def _():
         pl.semaphore_wait(barrier, n_src - 1)
-        pl.semaphore_signal(group_sem, 1, device_id={"src": leader})
-
-    @pl.when(src == leader)
-    def _():
-        pl.semaphore_wait(group_sem, n_src - 1)
-
-        @pl.loop(0, n_blk - 1)
-        def _(step):
-            pl.semaphore_signal(barrier, 1, device_id={"blk": far_first(step)})
+        for peer in range(1, n_src):
+            pl.semaphore_signal(group_sem, 1, device_id={"src": peer})
+
+    @pl.when(src != hub)
+    def _():
+        pl.semaphore_wait(group_sem, 1)
 
     def to_src(source, target, sem):
         copies = []
@@ -166,12 +169,43 @@
         return copies
 
     def to_blk(source, target, sem):
-        @pl.loop(0, n_blk - 1)
-        def _(step):
-            peer = far_first(step)
+        for peer in others:
             pltpu.make_async_remote_copy(
                 src_ref=source(peer), dst_ref=target.at[blk],
                 send_sem=sem.at[0], recv_sem=sem.at[1], device_id={"blk": peer}).start()
+
+    left, right, across = (src - 1) % n_src, (src + 1) % n_src, (src + 2) % n_src
+    half = share // 2
+    halves = pl.ds(0, half), pl.ds(half, half)
+
+    def pass_copy(source, target, step, k):
+        return pltpu.make_async_remote_copy(
+            src_ref=source, dst_ref=target, send_sem=part_sem.at[0, k], recv_sem=part_sem.at[1, k],
+            device_id={"src": (src + step) % n_src})
+
+    def piece(chunk, h):
+        return vals.at[pl.ds(pl.multiple_of(chunk * share + h * half, half), half)]
+
+    scattered = (
+        pass_copy(piece(across, 0), hold.at[0], 1, 0), pass_copy(piece(across, 1), hold.at[1], -1, 1),
+        pass_copy(piece(right, 1), hold.at[2], 1, 2), pass_copy(piece(left, 0), hold.at[3], -1, 3))
+    paired = pass_copy(hold.at[4], hold.at[6], 1, 4), pass_copy(hold.at[5], hold.at[7], -1, 5)
+
+    def scatter():
+        for copy in scattered:
+            copy.start()
+
+    def pair():
+        for copy in scattered:
+            copy.wait()
+
+        @pl.loop(0, half)
+        def _(k):
+            hold[4, k] = vals[right * share + k] + hold[0, k]
+            hold[5, k] = vals[left * share + half + k] + hold[1, k]
+
+        for copy in paired:
+            copy.start()
 
     def ring_copy(chunk, part, step, k):
         block = full.at[chunk, part] if part is not None else full.at[chunk]
@@ -183,20 +217,21 @@
         most = buffer.at[pl.ds(0, n_blk - 1)]
         pltpu.make_async_copy(most, most, sem).wait()
 
-    def through_owners(e, lines, follow, meanwhile=lambda: None):
+    def through_owners(e, lines, follow, after_first, after_second):
         slot_out[e] = pick(to_slots, lines).reshape(n_blk, 2, rows)
         to_blk(lambda peer: slot_out.at[e, peer], slot_in.at[e], slot_sem.at[e])
+        after_first()
         slot_in[e, blk] = slot_out[e, blk]
         if follow is None:
             all_of(meta_all, meta_sem.at[1])
             follow = successor(
                 meta_all[:, 0, :].astype(jnp.float32), meta_all[:, 1, :].astype(jnp.float32),
                 blk, tiles, key_count)
-        meanwhile()
         all_of(slot_in.at[e], slot_sem.at[e, 1])
         next_out[e] = pick(follow, slot_in[e].reshape(slots, rows)).reshape(n_blk, 2, rows)
         to_blk(lambda peer: next_out.at[e, peer], next_in.at[e], next_sem.at[e])
         next_in[e, blk] = next_out[e, blk]
+        after_second()
         return follow
 
     def from_owners(e):
@@ -204,18 +239,18 @@
         there[...] = pick(from_slots, next_in[e].reshape(slots, rows))
 
     share_copies = to_src(lambda peer: shares.at[src], shares.at[src], share_sem)
-    part_copies = to_src(
-        lambda peer: vals.at[pl.ds(pl.multiple_of(peer * share, share), share)], parts.at[src], part_sem)
-
-    @pl.when(src == leader)
+    @pl.when(src == hub)
+    def _():
+        pl.semaphore_wait(open_sem, 1)
+
+    @pl.when(src == relay)
+    def _():
+        pl.semaphore_wait(barrier, 2 * (n_blk - 1))
+        pl.semaphore_signal(open_sem, 1, device_id={"src": hub})
+
+    @pl.when(src > relay)
     def _():
         pl.semaphore_wait(barrier, n_blk - 1)
-        for step in src_steps:
-            pl.semaphore_signal(open_sem, 1, device_id={"src": lax.rem(src + step, n_src)})
-
-    @pl.when(src != leader)
-    def _():
-        pl.semaphore_wait(open_sem, 1)
 
     to_blk(lambda peer: meta_own, meta_all, meta_sem)
     for copy in share_copies:
@@ -223,14 +258,15 @@
     fixed[0] = functools.reduce(jnp.add, [shares[s, 0] for s in range(n_src)])
     fixed[1] = functools.reduce(jnp.add, [shares[s, 1] for s in range(n_src)])
     here[...] = fixed[0] / fixed[1]
-    follow = through_owners(0, here[...], None)
-
-    for copy in part_copies:
+    follow = through_owners(0, here[...], None, scatter, pair)
+
+    for copy in paired:
         copy.wait()
 
-    @pl.loop(0, share)
+    @pl.loop(0, half)
     def _(k):
-        full[src, k] = functools.reduce(jnp.add, [parts[s, k] for s in range(n_src)])
+        full[src, k] = vals[src * share + k] + hold[3, k] + hold[6, k]
+        full[src, half + k] = vals[src * share + half + k] + hold[2, k] + hold[7, k]
 
     first = pl.multiple_of(src * share, share)
 
@@ -245,24 +281,24 @@
         total = near[at, :] + products(full.at[src], cols, there, g * 8, first + g * 8, rows)
         quarters[src, pl.ds(g * 8, 8), :] = (fixed[0, at, :] - total) / fixed[1, at, :]
     quarter_copies = to_src(lambda peer: quarters.at[src], quarters.at[src], quarter_sem)
-    to_right, to_left = ring_copy(src, None, 1, 0), ring_copy(src, None, -1, 1)
-    to_right.start()
-    to_left.start()
     for copy in quarter_copies:
         copy.wait()
     here[...] = quarters[...].reshape(tiles, rows)
 
-    left, right, across = (src - 1) % n_src, (src + 1) % n_src, (src + 2) % n_src
-    halves = pl.ds(0, share // 2), pl.ds(share // 2, share // 2)
+    gathered = ring_copy(src, None, 1, 0), ring_copy(src, None, -1, 1)
     onward = ring_copy(left, halves[0], 1, 2), ring_copy(right, halves[1], -1, 3)
 
+    def gather():
+        for copy in gathered:
+            copy.start()
+
     def pass_on():
-        to_right.wait()
-        onward[0].start()
-        to_left.wait()
-        onward[1].start()
-
-    through_owners(1, here[...], follow, pass_on)
+        for copy in gathered:
+            copy.wait()
+        for copy in onward:
+            copy.start()
+
+    through_owners(1, here[...], follow, gather, pass_on)
 
     def near_of(s):
         @pl.loop(0, share // 8)
@@ -319,19 +355,19 @@
                 pltpu.VMEM((steps, n_blk, 2, rows), row),
                 pltpu.VMEM((steps, n_blk, 2, rows), row),
                 pltpu.VMEM((steps, n_blk, 2, rows), row),
-                pltpu.VMEM((n_src, tiles // n_src, stored, rows), row),
+                pltpu.VMEM((8, tiles // n_src // 2, stored, rows), row),
                 pltpu.VMEM((n_src, tiles // n_src, stored, rows), row),
                 pltpu.VMEM((n_src, tiles // n_src, rows), row),
                 pltpu.VMEM((tiles, rows), row),
                 pltpu.VMEM((tiles, rows), row),
                 pltpu.VMEM((tiles, rows), row),
                 pltpu.VMEM((2, tiles, rows), row),
-                dma((8,)),
+                dma((7,)),
                 dma((2,)),
                 dma((2, n_src)),
                 dma((steps, 2)),
                 dma((steps, 2)),
-                dma((2, n_src)),
+                dma((2, 6)),
                 dma((2, 4)),
                 dma((2, n_src)),
                 pltpu.SemaphoreType.REGULAR,

time: 51.7 us -> 46 us (0.89)
  Pallas kernels: 50.8 us -> 45.3 us
    pallas_call x1, Pallas kernels: 50.8 us -> 45.3 us  [on_device(): pl.pallas_call(functools.partial(kernel, n_src, n_blk, grid, tiles, store...]
where the time goes in v4:
time: 46 us; the launch traced here: 45.9 us
  Pallas kernels  45.3 us (98%)
  local copies, waits for them, and re-layouts  0.62 us (1%)
    pallas_call x1, Pallas kernels, on_device(): pl.pallas_call(functools.partial(kernel, n_src, n_blk, grid, tiles, store...  45.3 us

profile of v4, /device:TPU:1, one launch (start us, length us, event | category | flops | bytes accessed | tf_op | source)
XLA Modules:
  0.0 45.9 jit_solution(17741020845445345003)
XLA Ops:
  0.0 45.3 %sweeps.1 = f32[64,128]{1,0:T(8,128)S(1)} custom-call(f32[1,64,32,128]{3,2,1,0:T(8,128)} %vals_in.1, s32[64,32,128]{2,1,0:T(8,128)} %cols_in.1, f32[1,64,128]{2,1,0:T(8,128)} %diag_in.1, f32[1,64,128]{2,1,0:T(8,128)} %rhs_in.1, s32[64,128]{1,0:T(8,128)} %map_in.1, s32[1,64]{1,0:T(1,128)} %bitcast.2, s32[1,64]{1,0:T(1,128)} %bitcast.3), custom_call_target="tpu_custom_call" | custom-call | tf_op jit(solution)/shard_map/sweeps/pallas_call | solution.py:338
  45.3 0.6 %copy.9 = f32[64,128]{1,0:T(8,128)} copy(f32[64,128]{1,0:T(8,128)S(1)} %sweeps.1) | data formatting | bytes 65536

commit v5 on v4

--- a/solution.py
+++ b/solution.py
@@ -191,12 +191,8 @@
         pass_copy(piece(right, 1), hold.at[2], 1, 2), pass_copy(piece(left, 0), hold.at[3], -1, 3))
     paired = pass_copy(hold.at[4], hold.at[6], 1, 4), pass_copy(hold.at[5], hold.at[7], -1, 5)
 
-    def scatter():
-        for copy in scattered:
-            copy.start()
-
     def pair():
-        for copy in scattered:
+        for copy in scattered[:2]:
             copy.wait()
 
         @pl.loop(0, half)
@@ -204,7 +200,7 @@
             hold[4, k] = vals[right * share + k] + hold[0, k]
             hold[5, k] = vals[left * share + half + k] + hold[1, k]
 
-        for copy in paired:
+        for copy in (*paired, *scattered[2:]):
             copy.start()
 
     def ring_copy(chunk, part, step, k):
@@ -255,12 +251,14 @@
     to_blk(lambda peer: meta_own, meta_all, meta_sem)
     for copy in share_copies:
         copy.wait()
+    for copy in scattered[:2]:
+        copy.start()
     fixed[0] = functools.reduce(jnp.add, [shares[s, 0] for s in range(n_src)])
     fixed[1] = functools.reduce(jnp.add, [shares[s, 1] for s in range(n_src)])
     here[...] = fixed[0] / fixed[1]
-    follow = through_owners(0, here[...], None, scatter, pair)
-
-    for copy in paired:
+    follow = through_owners(0, here[...], None, pair, lambda: None)
+
+    for copy in (*scattered[2:], *paired):
         copy.wait()
 
     @pl.loop(0, half)

time: 46 us -> 44.9 us (0.976)
  Pallas kernels: 45.3 us -> 44.1 us
    pallas_call x1, Pallas kernels: 45.3 us -> 44.1 us  [on_device(): pl.pallas_call(functools.partial(kernel, n_src, n_blk, grid, tiles, store...]
where the time goes in v5:
time: 44.9 us; the launch traced here: 44.8 us
  Pallas kernels  44.1 us (98%)
  local copies, waits for them, and re-layouts  0.62 us (1%)
    pallas_call x1, Pallas kernels, on_device(): pl.pallas_call(functools.partial(kernel, n_src, n_blk, grid, tiles, store...  44.1 us

profile of v5, /device:TPU:1, one launch (start us, length us, event | category | flops | bytes accessed | tf_op | source)
XLA Modules:
  0.0 44.8 jit_solution(8857131423538962653)
XLA Ops:
  0.0 44.1 %sweeps.1 = f32[64,128]{1,0:T(8,128)S(1)} custom-call(f32[1,64,32,128]{3,2,1,0:T(8,128)} %vals_in.1, s32[64,32,128]{2,1,0:T(8,128)} %cols_in.1, f32[1,64,128]{2,1,0:T(8,128)} %diag_in.1, f32[1,64,128]{2,1,0:T(8,128)} %rhs_in.1, s32[64,128]{1,0:T(8,128)} %map_in.1, s32[1,64]{1,0:T(1,128)} %bitcast.2, s32[1,64]{1,0:T(1,128)} %bitcast.3), custom_call_target="tpu_custom_call" | custom-call | tf_op jit(solution)/shard_map/sweeps/pallas_call | solution.py:336
  44.1 0.6 %copy.9 = f32[64,128]{1,0:T(8,128)} copy(f32[64,128]{1,0:T(8,128)S(1)} %sweeps.1) | data formatting | bytes 65536

commit v6 on v5

--- a/solution.py
+++ b/solution.py
@@ -24,17 +24,22 @@
     return jnp.sum(square, axis=1, keepdims=True)
 
 
+def slot_numbers(owner_row, tiles, slots):
+    row_at, col_at = iota((tiles, tiles), 0), iota((tiles, tiles), 1)
+    owner_col = jnp.sum(jnp.where(row_at == col_at, owner_row, 0), axis=1, keepdims=True)
+    earlier = (owner_col == owner_row) & (row_at < col_at)
+    before = jnp.sum(jnp.where(earlier, 1, 0), axis=0, keepdims=True)
+    return jnp.minimum(2 * owner_row + jnp.minimum(before, 1), slots - 1)
+
+
 def source_slots(owner_row, tiles, slots):
     owner_col = turned(owner_row, tiles)
     same = owner_col == owner_row
     row_at, col_at = iota((tiles, tiles), 0), iota((tiles, tiles), 1)
-    before_col = jnp.sum(jnp.where(same & (col_at < row_at), 1.0, 0.0), axis=1, keepdims=True)
     before_row = jnp.sum(jnp.where(same & (row_at < col_at), 1.0, 0.0), axis=0, keepdims=True)
-    slot_col = 2.0 * owner_col + before_col
     slot_row = 2.0 * owner_row + before_row
     to_slots = jnp.where(iota((slots, tiles), 0).astype(jnp.float32) == slot_row, 1.0, 0.0)
-    from_slots = jnp.where(iota((tiles, slots), 1).astype(jnp.float32) == slot_col, 1.0, 0.0)
-    return to_slots, from_slots
+    return to_slots
 
 
 def successor(owners, keys, me, tiles, key_count):
@@ -72,11 +77,11 @@
     return parts[0]
 
 
-def products(vals, cols, lines, v0, t0, bit):
+def products(vals, cols, line_of, v0, t0, bit):
     _, stored, rows = cols.shape
     parts = []
     for k in range(8):
-        line = jnp.broadcast_to(lines[pl.ds(t0 + k, 1), :], (8, rows))
+        line = jnp.broadcast_to(line_of(t0 + k), (8, rows))
         total = None
         for j in range(stored // 8):
             code = cols[t0 + k, pl.ds(8 * j, 8), :]
@@ -92,8 +97,8 @@
     vals_in, cols_in, diag_in, rhs_in, map_in, dest_in, keys_in, out,
     vals, cols, diag, rhs, owner_map, dest, keys,
     meta_own, meta_all, shares, slot_out, slot_in, next_out, next_in,
-    hold, full, quarters, here, there, near, fixed,
-    load_sem, meta_sem, share_sem, slot_sem, next_sem, part_sem, full_sem, quarter_sem, group_sem, open_sem,
+    hold, full, quarters, here, near, fixed, slot_row, slot_at,
+    load_sem, meta_sem, share_sem, slot_sem, next_sem, part_sem, full_sem, quarter_sem, group_sem, open_sem, scalar_sem,
 ):
     src, blk = lax.axis_index("src"), lax.axis_index("blk")
     slots = 2 * n_blk
@@ -139,13 +144,17 @@
     meta_own[0:1, 0:tiles] = dest[...]
     meta_own[1:2, 0:tiles] = keys[...]
     meta_all[blk] = meta_own[...]
-    to_slots, from_slots = source_slots(dest[...].astype(jnp.float32), tiles, slots)
+    slot_row[...] = slot_numbers(dest[...], tiles, slots)
+    to_slots = source_slots(dest[...].astype(jnp.float32), tiles, slots)
+    to_scalars = pltpu.make_async_copy(slot_row, slot_at, scalar_sem)
+    to_scalars.start()
     for load in loads[2:5]:
         load.wait()
     shares[src, 0] = jnp.where(owner_map[...] == src, rhs[...], 0.0)
     shares[src, 1] = diag[...]
     for load in loads[5:]:
         load.wait()
+    to_scalars.wait()
 
     @pl.when(src == hub)
     def _():
@@ -230,9 +239,18 @@
         after_second()
         return follow
 
+    def own_line(tile):
+        return here[pl.ds(tile, 1), :]
+
+    def next_line(e):
+        def line_of(tile):
+            slot = slot_at[0, tile]
+            return next_in[e, slot >> 1, pl.ds(slot & 1, 1), :]
+
+        return line_of
+
     def from_owners(e):
         all_of(next_in.at[e], next_sem.at[e, 1])
-        there[...] = pick(from_slots, next_in[e].reshape(slots, rows))
 
     share_copies = to_src(lambda peer: shares.at[src], shares.at[src], share_sem)
     @pl.when(src == hub)
@@ -271,12 +289,12 @@
     @pl.loop(0, share // 8)
     def _(g):
         near[pl.ds(pl.multiple_of(first + g * 8, 8), 8), :] = products(
-            full.at[src], cols, here, g * 8, first + g * 8, 0)
+            full.at[src], cols, own_line, g * 8, first + g * 8, 0)
 
     from_owners(0)
     for g in range(share // 8):
         at = pl.ds(pl.multiple_of(first + g * 8, 8), 8)
-        total = near[at, :] + products(full.at[src], cols, there, g * 8, first + g * 8, rows)
+        total = near[at, :] + products(full.at[src], cols, next_line(0), g * 8, first + g * 8, rows)
         quarters[src, pl.ds(g * 8, 8), :] = (fixed[0, at, :] - total) / fixed[1, at, :]
     quarter_copies = to_src(lambda peer: quarters.at[src], quarters.at[src], quarter_sem)
     for copy in quarter_copies:
@@ -302,7 +320,7 @@
         @pl.loop(0, share // 8)
         def _(g):
             start = s * share + g * 8
-            near[pl.ds(pl.multiple_of(start, 8), 8), :] = products(full.at[s], cols, here, g * 8, start, 0)
+            near[pl.ds(pl.multiple_of(start, 8), 8), :] = products(full.at[s], cols, own_line, g * 8, start, 0)
 
     for chunk in (src, left, right):
         near_of(chunk)
@@ -313,7 +331,7 @@
     for s in range(n_src):
         for g in range(share // 8):
             at = pl.ds(s * share + g * 8, 8)
-            total = near[at, :] + products(full.at[s], cols, there, g * 8, s * share + g * 8, rows)
+            total = near[at, :] + products(full.at[s], cols, next_line(1), g * 8, s * share + g * 8, rows)
             out[at, :] = (fixed[0, at, :] - total) / fixed[1, at, :]
 
     all_of(meta_all, meta_sem.at[0])
@@ -358,8 +376,9 @@
                 pltpu.VMEM((n_src, tiles // n_src, rows), row),
                 pltpu.VMEM((tiles, rows), row),
                 pltpu.VMEM((tiles, rows), row),
-                pltpu.VMEM((tiles, rows), row),
                 pltpu.VMEM((2, tiles, rows), row),
+                pltpu.VMEM((1, tiles), jnp.int32),
+                pltpu.SMEM((1, tiles), jnp.int32),
                 dma((7,)),
                 dma((2,)),
                 dma((2, n_src)),
@@ -370,6 +389,7 @@
                 dma((2, n_src)),
                 pltpu.SemaphoreType.REGULAR,
                 pltpu.SemaphoreType.REGULAR,
+                dma,
             ],
             compiler_params=pltpu.CompilerParams(collective_id=0, has_side_effects=True),
             name="sweeps",

time: 44.9 us -> 44.4 us (0.989)
  no operation moved by 1% of the time
where the time goes in v6:
time: 44.4 us; the launch traced here: 44.3 us
  Pallas kernels  43.7 us (98%)
  local copies, waits for them, and re-layouts  0.62 us (1%)
    pallas_call x1, Pallas kernels, on_device(): pl.pallas_call(functools.partial(kernel, n_src, n_blk, grid, tiles, store...  43.7 us

profile of v6, /device:TPU:1, one launch (start us, length us, event | category | flops | bytes accessed | tf_op | source)
XLA Modules:
  0.0 44.3 jit_solution(16684721681473857507)
XLA Ops:
  0.0 43.7 %sweeps.1 = f32[64,128]{1,0:T(8,128)S(1)} custom-call(f32[1,64,32,128]{3,2,1,0:T(8,128)} %vals_in.1, s32[64,32,128]{2,1,0:T(8,128)} %cols_in.1, f32[1,64,128]{2,1,0:T(8,128)} %diag_in.1, f32[1,64,128]{2,1,0:T(8,128)} %rhs_in.1, s32[64,128]{1,0:T(8,128)} %map_in.1, s32[1,64]{1,0:T(1,128)} %bitcast.2, s32[1,64]{1,0:T(1,128)} %bitcast.3), custom_call_target="tpu_custom_call" | custom-call | tf_op jit(solution)/shard_map/sweeps/pallas_call | solution.py:354
  43.7 0.6 %copy.9 = f32[64,128]{1,0:T(8,128)} copy(f32[64,128]{1,0:T(8,128)S(1)} %sweeps.1) | data formatting | bytes 65536

commit v7 on v6

--- a/solution.py
+++ b/solution.py
@@ -86,7 +86,8 @@
         for j in range(stored // 8):
             code = cols[t0 + k, pl.ds(8 * j, 8), :]
             near = jnp.take_along_axis(line, code & (rows - 1), axis=1, mode="promise_in_bounds")
-            term = jnp.where((code & rows) == bit, vals[v0 + k, pl.ds(8 * j, 8), :], 0.0) * near
+            value = vals[v0 + k, pl.ds(8 * j, 8), :]
+            term = (value if bit is None else jnp.where((code & rows) == bit, value, 0.0)) * near
             total = term if total is None else total + term
         parts.append(total)
     return folded(parts)
@@ -321,6 +322,8 @@
         def _(g):
             start = s * share + g * 8
             near[pl.ds(pl.multiple_of(start, 8), 8), :] = products(full.at[s], cols, own_line, g * 8, start, 0)
+            for k in range(8):
+                vals[start + k] = jnp.where((cols[start + k] & rows) == rows, full[s, g * 8 + k], 0.0)
 
     for chunk in (src, left, right):
         near_of(chunk)
@@ -331,7 +334,7 @@
     for s in range(n_src):
         for g in range(share // 8):
             at = pl.ds(s * share + g * 8, 8)
-            total = near[at, :] + products(full.at[s], cols, next_line(1), g * 8, s * share + g * 8, rows)
+            total = near[at, :] + products(vals, cols, next_line(1), s * share + g * 8, s * share + g * 8, None)
             out[at, :] = (fixed[0, at, :] - total) / fixed[1, at, :]
 
     all_of(meta_all, meta_sem.at[0])

time: 44.4 us -> 44.4 us (level)
  no operation moved by 1% of the time
where the time goes in v7:
time: 44.4 us; the launch traced here: 44.3 us
  Pallas kernels  43.7 us (98%)
  local copies, waits for them, and re-layouts  0.62 us (1%)
    pallas_call x1, Pallas kernels, on_device(): pl.pallas_call(functools.partial(kernel, n_src, n_blk, grid, tiles, store...  43.7 us

profile of v7, /device:TPU:1, one launch (start us, length us, event | category | flops | bytes accessed | tf_op | source)
XLA Modules:
  0.0 44.3 jit_solution(6236153417319696780)
XLA Ops:
  0.0 43.7 %sweeps.1 = f32[64,128]{1,0:T(8,128)S(1)} custom-call(f32[1,64,32,128]{3,2,1,0:T(8,128)} %vals_in.1, s32[64,32,128]{2,1,0:T(8,128)} %cols_in.1, f32[1,64,128]{2,1,0:T(8,128)} %diag_in.1, f32[1,64,128]{2,1,0:T(8,128)} %rhs_in.1, s32[64,128]{1,0:T(8,128)} %map_in.1, s32[1,64]{1,0:T(1,128)} %bitcast.2, s32[1,64]{1,0:T(1,128)} %bitcast.3), custom_call_target="tpu_custom_call" | custom-call | tf_op jit(solution)/shard_map/sweeps/pallas_call | solution.py:357
  43.7 0.6 %copy.9 = f32[64,128]{1,0:T(8,128)} copy(f32[64,128]{1,0:T(8,128)S(1)} %sweeps.1) | data formatting | bytes 65536
